TPU v7x, 256 devices: a whole 4x4x8 slice. The times are simulated.
256 devices in a mesh: row: 8 (over y, core), col: 32 (over z, x).
Axes of the slice: x: 4, y: 4, z: 8, core: 2. Of those that a mesh axis runs over, the one named last changes fastest.
Arguments:
- rhs: bfloat16 [6144, 6144], P('row', 'col'), may hold values from -6 to 6
- basis_left: bfloat16 [6144, 6144], P('col', 'row'), may hold values from -1 to 1, as said below
- basis_right: bfloat16 [6144, 6144], P('row', 'col'), may hold values from -1 to 1, as said below
- eig_left: float32 [6144], P('row'), may hold values from 0.1 to 4
- eig_right: float32 [6144], P('col'), may hold values from 0.1 to 4
Outputs:
- solution: bfloat16 [6144, 6144], P('col', 'row')
Inputs may be any that keep to these rules, and one draw needn't show every extreme that they name: `basis_left`: an orthogonal matrix drawn uniformly, rounded to bfloat16. `basis_right`: an orthogonal matrix drawn uniformly, rounded to bfloat16.
All inputs are finite; a program needn't handle non-finite values.
Results may differ from a plain program's by a relative error of at most 0.0085.
Values may be sent and summed in bfloat16 or wider, within the bound.
No kernel may reach another device: no remote copies, remote signals or barrier semaphores. Data moves between devices by JAX's collectives and lax.ppermute only.
A program may use at most 64 MiB of HBM per device.

v0:
```python
import jax
import jax.numpy as jnp
from jax import lax
from jax.sharding import Mesh, PartitionSpec as P

F32, BF16 = (jnp.float32, jnp.bfloat16)
ROW = ("y", "core")


def dot(a, b, over):
    return lax.dot_general(a, b, ((over[:1], over[1:]), ((), ())), preferred_element_type=F32)


def gathered(shard, axis, dim):
    copies = jnp.broadcast_to(shard, (lax.axis_size(axis), *shard.shape))
    parts = lax.all_to_all(copies, axis, 0, 0, tiled=True)
    if dim == 0:
        return parts.reshape(-1, parts.shape[-1])
    return jnp.moveaxis(parts, 0, 1).reshape(parts.shape[1], -1)


def summed(partial, axis):
    peers = lax.axis_size(axis)
    parts = partial.reshape(peers, partial.shape[0] // peers, partial.shape[1])
    parts = lax.all_to_all(parts, axis, 0, 0, tiled=True)
    return jnp.sum(parts.astype(F32), axis=0)


def body(rhs, basis_left, basis_right, eig_left, eig_right):
    row_of = [(z * 8 + r, r * 8 + z) for z in range(8) for r in range(8)]
    left = lax.all_gather(basis_left, "z", axis=0, tiled=True)
    c_part = lax.all_to_all(rhs, "x", 0, 1, tiled=True)
    c_block = gathered(c_part, ROW, 0)
    turned = lax.ppermute(basis_right, (*ROW, "z"), row_of)
    right = lax.all_gather(turned, ROW, axis=1, tiled=True)
    part = dot(left, c_block, (0, 0)).astype(BF16)
    projected = gathered(summed(part, "x").astype(BF16), "x", 0)
    part = dot(projected, right, (1, 0)).astype(BF16)
    second = lax.psum_scatter(part, "z", scatter_dimension=1, tiled=True).astype(F32)
    scaled = (second / (eig_left[:, None] + eig_right[None, :])).astype(BF16)
    basis_right, _ = lax.optimization_barrier((basis_right, part))
    right = lax.all_gather(basis_right, "x", axis=1, tiled=True)
    scaled = gathered(scaled, "x", 1)
    part = dot(left, scaled, (1, 0)).astype(BF16)
    half = summed(part, "core").astype(BF16)
    half = summed(half, "y").astype(BF16)
    half = gathered(gathered(half, "y", 0), "core", 0)
    part = dot(half, right, (1, 1)).astype(BF16)
    return lax.psum_scatter(part, "z", scatter_dimension=0, tiled=True)


def solution(mesh):
    split = Mesh(mesh.devices.reshape(4, 2, 8, 4), ("y", "core", "z", "x"))
    row, col = (ROW, ("z", "x"))
    in_specs = (P(row, col), P(col, row), P(row, col), P(row), P(col))
    return jax.shard_map(
        body, mesh=split, in_specs=in_specs, out_specs=P(col, row), check_vma=False
    )
```

profile of v0, /device:TPU:14, one launch (start us, length us, event | category | flops | bytes accessed | tf_op | source)
XLA Modules:
  0.0 283.0 jit_solution(11018644528555109359)
XLA Ops:
  7.3 1.9 copy.19
  9.1 4.8 %all-to-all-start = ((bf16[4,192,192]{2,1,0:T(8,128)(2,1)}), bf16[4,192,192]{2,1,0:T(8,128)(2,1)S(1)}, u32[]{:S(2)}, u32[]{:S(2)}) async-start(bf16[4,192,192]{2,1,0:T(8,128)(2,1)} %bitcast), calls=%async_computation | async-start | bytes 786432 | tf_op jit(solution)/shard_map/all_to_all | solution.py:32
  13.9 5.1 %collective-permute-start = (bf16[768,192]{0,1:T(8,128)(2,1)}, bf16[768,192]{0,1:T(8,128)(2,1)S(1)}, u32[]{:S(2)}, u32[]{:S(2)}) collective-permute-start(bf16[768,192]{0,1:T(8,128)(2,1)} %param.7), channel_id=1, source_target_pairs={{0,0},{4,32},{8,64},{12,96},{16,128},{20,160},{24,192},{28,224},{3... | collective-permute-start | bytes 884744 | tf_op jit(solution)/shard_map/ppermute | solution.py:34
  22.2 7.8 %all-to-all-start.1 = ((bf16[8,192,768]{2,1,0:T(8,128)(2,1)}), bf16[8,192,768]{2,1,0:T(8,128)(2,1)S(1)}, u32[]{:S(2)}, u32[]{:S(2)}) async-start(bf16[8,192,768]{2,1,0:T(8,128)(2,1)} %broadcast_in_dim.17), calls=%async_computation.1 | async-start | bytes 4718592 | tf_op jit(solution)/shard_map/all_to_all | solution.py:16
  30.0 16.2 %collective-permute-done = bf16[768,192]{0,1:T(8,128)(2,1)S(1)} collective-permute-done((bf16[768,192]{0,1:T(8,128)(2,1)}, bf16[768,192]{0,1:T(8,128)(2,1)S(1)}, u32[]{:S(2)}, u32[]{:S(2)}) %collective-permute-start) | collective-permute-done | bytes 294944 | tf_op jit(solution)/shard_map/ppermute | solution.py:34
  47.0 11.5 %all-to-all-done.1 = bf16[8,192,768]{2,1,0:T(8,128)(2,1)S(1)} async-done(((bf16[8,192,768]{2,1,0:T(8,128)(2,1)}), bf16[8,192,768]{2,1,0:T(8,128)(2,1)S(1)}, u32[]{:S(2)}, u32[]{:S(2)}) %all-to-all-start.1) | async-done | bytes 2359328 | tf_op jit(solution)/shard_map/all_to_all | solution.py:16
  58.5 8.3 %all-gather.4.cloned.1.call-done = bf16[1536,768]{1,0:T(8,128)(2,1)} async-done(((bf16[192,768]{1,0:T(8,128)(2,1)}), bf16[1536,768]{1,0:T(8,128)(2,1)}) %all-gather.4.cloned.1.call-update) | async-done | bytes 2359312 | tf_op jit(solution)/shard_map/all_gather | solution.py:31
  66.8 3.7 %convolution_convert_fusion.3 = bf16[768,768]{1,0:T(8,128)(2,1)S(1)} fusion(bf16[1536,768]{1,0:T(8,128)(2,1)} %all-gather.4.cloned.1.call-done, bf16[1536,768]{1,0:T(8,128)(2,1)S(1)} %bitcast.30), kind=kOutput, calls=%fused_computation.4 | convolution fusion | flops 1812529152 | bytes 5898240 | tf_op jit(solution)/shard_map/dot_general | solution.py:11
  70.5 16.7 %all_to_all.59 = bf16[4,192,768]{2,1,0:T(8,128)(2,1)S(1)} all-to-all(bf16[4,192,768]{2,1,0:T(8,128)(2,1)S(1)} %bitcast.36), channel_id=1, replica_groups=mesh['y'=4,'core'=2,'z'=8,'x'=4] {'x'}, dimensions={0} | all-to-all | bytes 2359296 | tf_op jit(solution)/shard_map/all_to_all | solution.py:25
  88.6 5.6 %all-to-all-start.3 = ((bf16[4,192,768]{2,1,0:T(8,128)(2,1)}), bf16[4,192,768]{2,1,0:T(8,128)(2,1)S(1)}, u32[]{:S(2)}, u32[]{:S(2)}) async-start(bf16[4,192,768]{2,1,0:T(8,128)(2,1)} %broadcast_in_dim.18), calls=%async_computation.3 | async-start | bytes 2359296 | tf_op jit(solution)/shard_map/all_to_all | solution.py:16
  95.2 10.2 %all-to-all-done.3 = bf16[4,192,768]{2,1,0:T(8,128)(2,1)S(1)} async-done(((bf16[4,192,768]{2,1,0:T(8,128)(2,1)}), bf16[4,192,768]{2,1,0:T(8,128)(2,1)S(1)}, u32[]{:S(2)}, u32[]{:S(2)}) %all-to-all-start.3) | async-done | bytes 1179680 | tf_op jit(solution)/shard_map/all_to_all | solution.py:16
  105.4 3.7 %convolution_convert_fusion.2 = bf16[768,1536]{1,0:T(8,128)(2,1)S(1)} fusion(bf16[768,768]{1,0:T(8,128)(2,1)S(1)} %bitcast.34, bf16[768,1536]{0,1:T(8,128)(2,1)} %all-gather.6.cloned.1.call-done), kind=kOutput, calls=%fused_computation.2 | convolution fusion | flops 1813118976 | bytes 5898240 | tf_op jit(solution)/shard_map/dot_general | solution.py:11
  109.1 2.5 copy.25
  111.6 44.1 %reduce-scatter.7.cloned.1.call-done = bf16[192,768]{1,0:T(8,128)(2,1)} async-done(((bf16[1536,768]{1,0:T(8,128)(2,1)}), bf16[192,768]{1,0:T(8,128)(2,1)}) %reduce-scatter.7.cloned.1.call-update) | async-done | bytes 294928
  156.9 14.7 %all_to_all.60 = bf16[4,768,192]{1,2,0:T(8,128)(2,1)S(1)} all-to-all(bf16[4,768,192]{1,2,0:T(8,128)(2,1)S(1)} %broadcast_in_dim.19), channel_id=1, replica_groups=mesh['y'=4,'core'=2,'z'=8,'x'=4] {'x'}, dimensions={0} | all-to-all | bytes 2359296 | tf_op jit(solution)/shard_map/all_to_all | solution.py:16
  171.6 2.0 convolution_convert_fusion.1
  173.8 5.6 %all_to_all.61 = bf16[2,768,768]{1,2,0:T(8,128)(2,1)S(1)} all-to-all(bf16[2,768,768]{1,2,0:T(8,128)(2,1)S(1)} %bitcast.28), channel_id=1, replica_groups=mesh['y'=4,'core'=2,'z'=8,'x'=4] {'core'}, dimensions={0} | all-to-all | bytes 4718592 | tf_op jit(solution)/shard_map/all_to_all | solution.py:25
  182.1 4.8 %all-to-all-start.6 = ((bf16[4,192,768]{2,1,0:T(8,128)(2,1)}), bf16[4,192,768]{2,1,0:T(8,128)(2,1)S(1)}, u32[]{:S(2)}, u32[]{:S(2)}) async-start(bf16[4,192,768]{2,1,0:T(8,128)(2,1)} %bitcast.8), calls=%async_computation.6 | async-start | bytes 2359296 | tf_op jit(solution)/shard_map/all_to_all | solution.py:25
  187.4 14.8 %all-to-all-done.6 = bf16[4,192,768]{2,1,0:T(8,128)(2,1)S(1)} async-done(((bf16[4,192,768]{2,1,0:T(8,128)(2,1)}), bf16[4,192,768]{2,1,0:T(8,128)(2,1)S(1)}, u32[]{:S(2)}, u32[]{:S(2)}) %all-to-all-start.6) | async-done | bytes 1179680 | tf_op jit(solution)/shard_map/all_to_all | solution.py:25
  202.6 18.4 %all_to_all.62 = bf16[4,192,768]{2,1,0:T(8,128)(2,1)S(1)} all-to-all(bf16[4,192,768]{2,1,0:T(8,128)(2,1)S(1)} %broadcast_in_dim.20), channel_id=1, replica_groups=mesh['y'=4,'core'=2,'z'=8,'x'=4] {'y'}, dimensions={0} | all-to-all | bytes 2359296 | tf_op jit(solution)/shard_map/all_to_all | solution.py:16
  222.5 3.8 %all-to-all-start.8 = ((bf16[2,768,768]{2,1,0:T(8,128)(2,1)}), bf16[2,768,768]{2,1,0:T(8,128)(2,1)S(1)}, u32[]{:S(2)}, u32[]{:S(2)}) async-start(bf16[2,768,768]{2,1,0:T(8,128)(2,1)} %broadcast_in_dim.21), calls=%async_computation.8 | async-start | bytes 4718592 | tf_op jit(solution)/shard_map/all_to_all | solution.py:16
  226.4 3.0 %all-to-all-done.8 = bf16[2,768,768]{2,1,0:T(8,128)(2,1)S(1)} async-done(((bf16[2,768,768]{2,1,0:T(8,128)(2,1)}), bf16[2,768,768]{2,1,0:T(8,128)(2,1)S(1)}, u32[]{:S(2)}, u32[]{:S(2)}) %all-to-all-start.8) | async-done | bytes 2359328 | tf_op jit(solution)/shard_map/all_to_all | solution.py:16
  229.4 4.7 %convolution_convert_fusion = bf16[1536,768]{1,0:T(8,128)(2,1)} fusion(bf16[1536,768]{1,0:T(8,128)(2,1)S(1)} %bitcast.31, bf16[768,768]{0,1:T(8,128)(2,1)} %all-gather.8.cloned.1.call-done), kind=kOutput, calls=%fused_computation | convolution fusion | flops 1813118976 | bytes 5898240 | tf_op jit(solution)/shard_map/dot_general | solution.py:11
  234.1 42.3 %reduce-scatter.5.cloned.1.call-done = bf16[192,768]{1,0:T(8,128)(2,1)} async-done(((bf16[1536,768]{1,0:T(8,128)(2,1)}), bf16[192,768]{1,0:T(8,128)(2,1)}) %reduce-scatter.5.cloned.1.call-update) | async-done | bytes 294928 | tf_op jit(solution)/shard_map/reduce_scatter | solution.py:49
  (34 shorter events, 13.7 us)
Async XLA Ops:
  6.5 60.2 %all-gather.4.cloned.1.call-start = ((), (), s32[]{:S(2)}) async-start(), calls=%async_computation.11 | async-start | bytes 2654208 | tf_op jit(solution)/shard_map/all_gather | solution.py:31
  9.1 10.8 %all-to-all-start = ((bf16[4,192,192]{2,1,0:T(8,128)(2,1)}), bf16[4,192,192]{2,1,0:T(8,128)(2,1)S(1)}, u32[]{:S(2)}, u32[]{:S(2)}) async-start(bf16[4,192,192]{2,1,0:T(8,128)(2,1)} %bitcast), calls=%async_computation | async-start | bytes 786432 | tf_op jit(solution)/shard_map/all_to_all | solution.py:32
  13.9 32.3 %collective-permute-start = (bf16[768,192]{0,1:T(8,128)(2,1)}, bf16[768,192]{0,1:T(8,128)(2,1)S(1)}, u32[]{:S(2)}, u32[]{:S(2)}) collective-permute-start(bf16[768,192]{0,1:T(8,128)(2,1)} %param.7), channel_id=1, source_target_pairs={{0,0},{4,32},{8,64},{12,96},{16,128},{20,160},{24,192},{28,224},{3... | collective-permute-start | bytes 884744 | tf_op jit(solution)/shard_map/ppermute | solution.py:34
  22.2 36.3 %all-to-all-start.1 = ((bf16[8,192,768]{2,1,0:T(8,128)(2,1)}), bf16[8,192,768]{2,1,0:T(8,128)(2,1)S(1)}, u32[]{:S(2)}, u32[]{:S(2)}) async-start(bf16[8,192,768]{2,1,0:T(8,128)(2,1)} %broadcast_in_dim.17), calls=%async_computation.1 | async-start | bytes 4718592 | tf_op jit(solution)/shard_map/all_to_all | solution.py:16
  30.0 65.2 %all-gather.6.cloned.1.call-start = ((), (), s32[]{:S(2)}) async-start(), calls=%async_computation.12 | async-start | bytes 2654208 | tf_op jit(solution)/shard_map/all_gather | solution.py:35
  46.2 0.7 copy-start
  88.6 16.8 %all-to-all-start.3 = ((bf16[4,192,768]{2,1,0:T(8,128)(2,1)}), bf16[4,192,768]{2,1,0:T(8,128)(2,1)S(1)}, u32[]{:S(2)}, u32[]{:S(2)}) async-start(bf16[4,192,768]{2,1,0:T(8,128)(2,1)} %broadcast_in_dim.18), calls=%async_computation.3 | async-start | bytes 2359296 | tf_op jit(solution)/shard_map/all_to_all | solution.py:16
  94.1 61.6 %reduce-scatter.7.cloned.1.call-start = ((), (), s32[]{:S(2)}) async-start(), calls=%async_computation.15 | async-start | bytes 2654208
  111.5 44.2 %copy-start.1 = (f32[768]{0:T(1024)S(1)}, f32[768]{0:T(1024)}, u32[]{:S(2)}) copy-start(f32[768]{0:T(1024)} %param.8) | copy-start | bytes 9220
  111.5 44.2 %copy-start.2 = (f32[192]{0:T(256)S(1)}, f32[192]{0:T(256)}, u32[]{:S(2)}) copy-start(f32[192]{0:T(256)} %param.9) | copy-start | bytes 2308
  111.6 60.0 %copy-start.3 = (bf16[1536,768]{1,0:T(8,128)(2,1)S(1)}, bf16[1536,768]{1,0:T(8,128)(2,1)}, u32[]{:S(2)}) copy-start(bf16[1536,768]{1,0:T(8,128)(2,1)} %all-gather.4.cloned.1.call-done) | copy-start | bytes 7077892
  182.1 20.1 %all-to-all-start.6 = ((bf16[4,192,768]{2,1,0:T(8,128)(2,1)}), bf16[4,192,768]{2,1,0:T(8,128)(2,1)S(1)}, u32[]{:S(2)}, u32[]{:S(2)}) async-start(bf16[4,192,768]{2,1,0:T(8,128)(2,1)} %bitcast.8), calls=%async_computation.6 | async-start | bytes 2359296 | tf_op jit(solution)/shard_map/all_to_all | solution.py:25
  186.9 39.5 %all-gather.8.cloned.1.call-start = ((), (), s32[]{:S(2)}) async-start(), calls=%async_computation.13 | async-start | bytes 1474560 | tf_op jit(solution)/shard_map/all_gather | solution.py:42
  222.5 6.9 %all-to-all-start.8 = ((bf16[2,768,768]{2,1,0:T(8,128)(2,1)}), bf16[2,768,768]{2,1,0:T(8,128)(2,1)S(1)}, u32[]{:S(2)}, u32[]{:S(2)}) async-start(bf16[2,768,768]{2,1,0:T(8,128)(2,1)} %broadcast_in_dim.21), calls=%async_computation.8 | async-start | bytes 4718592 | tf_op jit(solution)/shard_map/all_to_all | solution.py:16
  226.3 50.1 %reduce-scatter.5.cloned.1.call-start = ((), (), s32[]{:S(2)}) async-start(), calls=%async_computation.14 | async-start | bytes 2654208 | tf_op jit(solution)/shard_map/reduce_scatter | solution.py:49
Sparse Core Ops, SparseCore 0:
  9.1 57.5 all-gather.3
  68.6 26.5 all-gather.5
  111.7 43.9 reduce-scatter.6
  189.2 25.5 all-gather.7
  234.2 42.1 reduce-scatter.4
where the time goes:
time: 284 us; the launch traced here: 283 us
  waiting for transfers between devices  154 us (54%)
  blocking collectives  55.4 us (20%)
  starting transfers between devices  31.8 us (11%)
  matrix products  14.1 us (5%)
  between operations  13.2 us (5%)
  local copies, waits for them, and re-layouts  11.8 us (4%)
  other arithmetic  2.88 us (1%)
    unnamed x6, waiting for transfers between devices  45.4 us
    reduce_scatter x1, waiting for transfers between devices, body(): return lax.psum_scatter(part, 'z', scatter_dimension=0, tiled=True)  42.3 us
    all_to_all x2, blocking collectives, gathered(): parts = lax.all_to_all(copies, axis, 0, 0, tiled=True)  33.1 us
    all_to_all x3, waiting for transfers between devices, gathered(): parts = lax.all_to_all(copies, axis, 0, 0, tiled=True)  24.7 us
    all_to_all x2, blocking collectives, summed(): parts = lax.all_to_all(parts, axis, 0, 0, tiled=True)  22.3 us
    all_to_all x3, starting transfers between devices, gathered(): parts = lax.all_to_all(copies, axis, 0, 0, tiled=True)  17.2 us
    ppermute x1, waiting for transfers between devices, body(): turned = lax.ppermute(basis_right, (*ROW, 'z'), row_of)  16.2 us
    all_to_all x1, waiting for transfers between devices, summed(): parts = lax.all_to_all(parts, axis, 0, 0, tiled=True)  14.8 us
  transfers between devices with their start and end apart: 11, of which 10 were waited for; matrix products, arithmetic and copies ran while one was open for 4% of the time, Pallas kernels for 0%

commit v1 on v0

--- a/solution.py
+++ b/solution.py
@@ -29,7 +29,9 @@
 def body(rhs, basis_left, basis_right, eig_left, eig_right):
     row_of = [(z * 8 + r, r * 8 + z) for z in range(8) for r in range(8)]
     left = lax.all_gather(basis_left, "z", axis=0, tiled=True)
-    c_part = lax.all_to_all(rhs, "x", 0, 1, tiled=True)
+    shards = jnp.split(rhs, lax.axis_size("x"), axis=0)
+    arrived = lax.all_to_all(jnp.stack(shards), "x", 0, 0)
+    c_part = jnp.concatenate(arrived, axis=1)
     c_block = gathered(c_part, ROW, 0)
     turned = lax.ppermute(basis_right, (*ROW, "z"), row_of)
     right = lax.all_gather(turned, ROW, axis=1, tiled=True)

time: 284 us -> 283 us (level)
  no operation moved by 1% of the time
where the time goes in v1:
time: 283 us; the launch traced here: 282 us
  waiting for transfers between devices  153 us (54%)
  blocking collectives  55 us (19%)
  starting transfers between devices  32.2 us (11%)
  matrix products  14.1 us (5%)
  between operations  13.2 us (5%)
  local copies, waits for them, and re-layouts  10.6 us (4%)
  other arithmetic  3.72 us (1%)
    unnamed x6, waiting for transfers between devices  45.7 us
    reduce_scatter x1, waiting for transfers between devices, body(): return lax.psum_scatter(part, 'z', scatter_dimension=0, tiled=True)  41.1 us
    all_to_all x2, blocking collectives, gathered(): parts = lax.all_to_all(copies, axis, 0, 0, tiled=True)  32.6 us
    all_to_all x3, waiting for transfers between devices, gathered(): parts = lax.all_to_all(copies, axis, 0, 0, tiled=True)  24.4 us
    all_to_all x2, blocking collectives, summed(): parts = lax.all_to_all(parts, axis, 0, 0, tiled=True)  22.3 us
    all_to_all x3, starting transfers between devices, gathered(): parts = lax.all_to_all(copies, axis, 0, 0, tiled=True)  17.2 us
    ppermute x1, waiting for transfers between devices, body(): turned = lax.ppermute(basis_right, (*ROW, 'z'), row_of)  16.5 us
    all_to_all x1, waiting for transfers between devices, summed(): parts = lax.all_to_all(parts, axis, 0, 0, tiled=True)  14.8 us
  transfers between devices with their start and end apart: 11, of which 10 were waited for; matrix products, arithmetic and copies ran while one was open for 4% of the time, Pallas kernels for 0%

profile of v1, /device:TPU:14, one launch (start us, length us, event | category | flops | bytes accessed | tf_op | source)
XLA Modules:
  0.0 281.9 jit_solution(1134754273605732889)
XLA Ops:
  9.3 4.8 %all-to-all-start = ((bf16[4,192,192]{1,2,0:T(8,128)(2,1)}), bf16[4,192,192]{1,2,0:T(8,128)(2,1)S(1)}, u32[]{:S(2)}, u32[]{:S(2)}) async-start(bf16[4,192,192]{1,2,0:T(8,128)(2,1)} %pad_maximum_fusion), calls=%async_computation | async-start | bytes 786432 | tf_op jit(solution)/shard_map/all_to_all | solution.py:33
  14.1 5.1 %collective-permute-start = (bf16[768,192]{0,1:T(8,128)(2,1)S(1)}, bf16[768,192]{0,1:T(8,128)(2,1)S(1)}, u32[]{:S(2)}, u32[]{:S(2)}) collective-permute-start(bf16[768,192]{0,1:T(8,128)(2,1)S(1)} %copy-done), channel_id=1, source_target_pairs={{0,0},{4,32},{8,64},{12,96},{16,128},{20,160},{24,192},{28,224},{3... | collective-permute-start | bytes 884744 | tf_op jit(solution)/shard_map/ppermute | solution.py:36
  20.2 1.6 broadcast_in_dim.17
  21.8 7.8 %all-to-all-start.1 = ((bf16[8,192,768]{2,1,0:T(8,128)(2,1)}), bf16[8,192,768]{2,1,0:T(8,128)(2,1)S(1)}, u32[]{:S(2)}, u32[]{:S(2)}) async-start(bf16[8,192,768]{2,1,0:T(8,128)(2,1)} %broadcast_in_dim.17), calls=%async_computation.1 | async-start | bytes 4718592 | tf_op jit(solution)/shard_map/all_to_all | solution.py:16
  29.6 16.5 %collective-permute-done = bf16[768,192]{0,1:T(8,128)(2,1)S(1)} collective-permute-done((bf16[768,192]{0,1:T(8,128)(2,1)S(1)}, bf16[768,192]{0,1:T(8,128)(2,1)S(1)}, u32[]{:S(2)}, u32[]{:S(2)}) %collective-permute-start) | collective-permute-done | bytes 294944 | tf_op jit(solution)/shard_map/ppermute | solution.py:36
  46.9 11.2 %all-to-all-done.1 = bf16[8,192,768]{2,1,0:T(8,128)(2,1)S(1)} async-done(((bf16[8,192,768]{2,1,0:T(8,128)(2,1)}), bf16[8,192,768]{2,1,0:T(8,128)(2,1)S(1)}, u32[]{:S(2)}, u32[]{:S(2)}) %all-to-all-start.1) | async-done | bytes 2359328 | tf_op jit(solution)/shard_map/all_to_all | solution.py:16
  58.1 8.6 %all-gather.4.cloned.1.call-done = bf16[1536,768]{1,0:T(8,128)(2,1)} async-done(((bf16[192,768]{1,0:T(8,128)(2,1)}), bf16[1536,768]{1,0:T(8,128)(2,1)}) %all-gather.4.cloned.1.call-update) | async-done | bytes 2359312 | tf_op jit(solution)/shard_map/all_gather | solution.py:31
  66.7 3.7 %convolution_convert_fusion.3 = bf16[768,768]{0,1:T(8,128)(2,1)S(1)} fusion(bf16[1536,768]{1,0:T(8,128)(2,1)S(1)} %bitcast.41, bf16[1536,768]{1,0:T(8,128)(2,1)} %all-gather.4.cloned.1.call-done), kind=kOutput, calls=%fused_computation.4 | convolution fusion | flops 1812529152 | bytes 5898240 | tf_op jit(solution)/shard_map/dot_general | solution.py:11
  70.4 16.7 %all_to_all.45 = bf16[4,192,768]{2,1,0:T(8,128)(2,1)S(1)} all-to-all(bf16[4,192,768]{2,1,0:T(8,128)(2,1)S(1)} %bitcast.47), channel_id=1, replica_groups=mesh['y'=4,'core'=2,'z'=8,'x'=4] {'x'}, dimensions={0} | all-to-all | bytes 2359296 | tf_op jit(solution)/shard_map/all_to_all | solution.py:25
  88.5 5.6 %all-to-all-start.3 = ((bf16[4,192,768]{2,1,0:T(8,128)(2,1)}), bf16[4,192,768]{2,1,0:T(8,128)(2,1)S(1)}, u32[]{:S(2)}, u32[]{:S(2)}) async-start(bf16[4,192,768]{2,1,0:T(8,128)(2,1)} %broadcast_in_dim.18), calls=%async_computation.3 | async-start | bytes 2359296 | tf_op jit(solution)/shard_map/all_to_all | solution.py:16
  95.2 10.2 %all-to-all-done.3 = bf16[4,192,768]{2,1,0:T(8,128)(2,1)S(1)} async-done(((bf16[4,192,768]{2,1,0:T(8,128)(2,1)}), bf16[4,192,768]{2,1,0:T(8,128)(2,1)S(1)}, u32[]{:S(2)}, u32[]{:S(2)}) %all-to-all-start.3) | async-done | bytes 1179680 | tf_op jit(solution)/shard_map/all_to_all | solution.py:16
  105.3 3.7 %convolution_convert_fusion.2 = bf16[768,1536]{1,0:T(8,128)(2,1)S(1)} fusion(bf16[768,768]{1,0:T(8,128)(2,1)S(1)} %bitcast.45, bf16[768,1536]{0,1:T(8,128)(2,1)} %all-gather.6.cloned.1.call-done), kind=kOutput, calls=%fused_computation.2 | convolution fusion | flops 1813118976 | bytes 5898240 | tf_op jit(solution)/shard_map/dot_general | solution.py:11
  109.0 2.4 copy.23
  111.5 44.4 %reduce-scatter.7.cloned.1.call-done = bf16[192,768]{1,0:T(8,128)(2,1)} async-done(((bf16[1536,768]{1,0:T(8,128)(2,1)}), bf16[192,768]{1,0:T(8,128)(2,1)}) %reduce-scatter.7.cloned.1.call-update) | async-done | bytes 294928
  157.1 14.3 %all_to_all.46 = bf16[4,768,192]{1,2,0:T(8,128)(2,1)S(1)} all-to-all(bf16[4,768,192]{1,2,0:T(8,128)(2,1)S(1)} %broadcast_in_dim.19), channel_id=1, replica_groups=mesh['y'=4,'core'=2,'z'=8,'x'=4] {'x'}, dimensions={0} | all-to-all | bytes 2359296 | tf_op jit(solution)/shard_map/all_to_all | solution.py:16
  171.4 2.0 convolution_convert_fusion.1
  173.6 5.6 %all_to_all.47 = bf16[2,768,768]{1,2,0:T(8,128)(2,1)S(1)} all-to-all(bf16[2,768,768]{1,2,0:T(8,128)(2,1)S(1)} %bitcast.39), channel_id=1, replica_groups=mesh['y'=4,'core'=2,'z'=8,'x'=4] {'core'}, dimensions={0} | all-to-all | bytes 4718592 | tf_op jit(solution)/shard_map/all_to_all | solution.py:25
  181.9 5.2 %all-to-all-start.6 = ((bf16[4,192,768]{2,1,0:T(8,128)(2,1)}), bf16[4,192,768]{2,1,0:T(8,128)(2,1)S(1)}, u32[]{:S(2)}, u32[]{:S(2)}) async-start(bf16[4,192,768]{2,1,0:T(8,128)(2,1)} %bitcast.13), calls=%async_computation.6 | async-start | bytes 2359296 | tf_op jit(solution)/shard_map/all_to_all | solution.py:25
  187.6 14.8 %all-to-all-done.6 = bf16[4,192,768]{2,1,0:T(8,128)(2,1)S(1)} async-done(((bf16[4,192,768]{2,1,0:T(8,128)(2,1)}), bf16[4,192,768]{2,1,0:T(8,128)(2,1)S(1)}, u32[]{:S(2)}, u32[]{:S(2)}) %all-to-all-start.6) | async-done | bytes 1179680 | tf_op jit(solution)/shard_map/all_to_all | solution.py:25
  202.7 18.4 %all_to_all.48 = bf16[4,192,768]{2,1,0:T(8,128)(2,1)S(1)} all-to-all(bf16[4,192,768]{2,1,0:T(8,128)(2,1)S(1)} %broadcast_in_dim.20), channel_id=1, replica_groups=mesh['y'=4,'core'=2,'z'=8,'x'=4] {'y'}, dimensions={0} | all-to-all | bytes 2359296 | tf_op jit(solution)/shard_map/all_to_all | solution.py:16
  222.7 3.8 %all-to-all-start.8 = ((bf16[2,768,768]{2,1,0:T(8,128)(2,1)}), bf16[2,768,768]{2,1,0:T(8,128)(2,1)S(1)}, u32[]{:S(2)}, u32[]{:S(2)}) async-start(bf16[2,768,768]{2,1,0:T(8,128)(2,1)} %broadcast_in_dim.21), calls=%async_computation.8 | async-start | bytes 4718592 | tf_op jit(solution)/shard_map/all_to_all | solution.py:16
  226.6 3.0 %all-to-all-done.8 = bf16[2,768,768]{2,1,0:T(8,128)(2,1)S(1)} async-done(((bf16[2,768,768]{2,1,0:T(8,128)(2,1)}), bf16[2,768,768]{2,1,0:T(8,128)(2,1)S(1)}, u32[]{:S(2)}, u32[]{:S(2)}) %all-to-all-start.8) | async-done | bytes 2359328 | tf_op jit(solution)/shard_map/all_to_all | solution.py:16
  229.5 4.7 %convolution_convert_fusion = bf16[1536,768]{1,0:T(8,128)(2,1)} fusion(bf16[1536,768]{1,0:T(8,128)(2,1)S(1)} %bitcast.42, bf16[768,768]{0,1:T(8,128)(2,1)} %all-gather.8.cloned.1.call-done), kind=kOutput, calls=%fused_computation | convolution fusion | flops 1813118976 | bytes 5898240 | tf_op jit(solution)/shard_map/dot_general | solution.py:11
  234.3 41.1 %reduce-scatter.5.cloned.1.call-done = bf16[192,768]{1,0:T(8,128)(2,1)} async-done(((bf16[1536,768]{1,0:T(8,128)(2,1)}), bf16[192,768]{1,0:T(8,128)(2,1)}) %reduce-scatter.5.cloned.1.call-update) | async-done | bytes 294928 | tf_op jit(solution)/shard_map/reduce_scatter | solution.py:51
  (36 shorter events, 13.6 us)
Async XLA Ops:
  6.5 7.5 %copy-start = (bf16[768,192]{0,1:T(8,128)(2,1)S(1)}, bf16[768,192]{0,1:T(8,128)(2,1)}, u32[]{:S(2)}) copy-start(bf16[768,192]{0,1:T(8,128)(2,1)} %param.7) | copy-start | bytes 884740
  6.5 60.2 %all-gather.4.cloned.1.call-start = ((), (), s32[]{:S(2)}) async-start(), calls=%async_computation.11 | async-start | bytes 2654208 | tf_op jit(solution)/shard_map/all_gather | solution.py:31
  9.3 10.8 %all-to-all-start = ((bf16[4,192,192]{1,2,0:T(8,128)(2,1)}), bf16[4,192,192]{1,2,0:T(8,128)(2,1)S(1)}, u32[]{:S(2)}, u32[]{:S(2)}) async-start(bf16[4,192,192]{1,2,0:T(8,128)(2,1)} %pad_maximum_fusion), calls=%async_computation | async-start | bytes 786432 | tf_op jit(solution)/shard_map/all_to_all | solution.py:33
  14.1 32.1 %collective-permute-start = (bf16[768,192]{0,1:T(8,128)(2,1)S(1)}, bf16[768,192]{0,1:T(8,128)(2,1)S(1)}, u32[]{:S(2)}, u32[]{:S(2)}) collective-permute-start(bf16[768,192]{0,1:T(8,128)(2,1)S(1)} %copy-done), channel_id=1, source_target_pairs={{0,0},{4,32},{8,64},{12,96},{16,128},{20,160},{24,192},{28,224},{3... | collective-permute-start | bytes 884744 | tf_op jit(solution)/shard_map/ppermute | solution.py:36
  21.8 36.3 %all-to-all-start.1 = ((bf16[8,192,768]{2,1,0:T(8,128)(2,1)}), bf16[8,192,768]{2,1,0:T(8,128)(2,1)S(1)}, u32[]{:S(2)}, u32[]{:S(2)}) async-start(bf16[8,192,768]{2,1,0:T(8,128)(2,1)} %broadcast_in_dim.17), calls=%async_computation.1 | async-start | bytes 4718592 | tf_op jit(solution)/shard_map/all_to_all | solution.py:16
  29.6 65.5 %all-gather.6.cloned.1.call-start = ((), (), s32[]{:S(2)}) async-start(), calls=%async_computation.12 | async-start | bytes 2654208 | tf_op jit(solution)/shard_map/all_gather | solution.py:37
  46.2 0.7 copy-start.1
  88.5 16.8 %all-to-all-start.3 = ((bf16[4,192,768]{2,1,0:T(8,128)(2,1)}), bf16[4,192,768]{2,1,0:T(8,128)(2,1)S(1)}, u32[]{:S(2)}, u32[]{:S(2)}) async-start(bf16[4,192,768]{2,1,0:T(8,128)(2,1)} %broadcast_in_dim.18), calls=%async_computation.3 | async-start | bytes 2359296 | tf_op jit(solution)/shard_map/all_to_all | solution.py:16
  94.1 61.8 %reduce-scatter.7.cloned.1.call-start = ((), (), s32[]{:S(2)}) async-start(), calls=%async_computation.15 | async-start | bytes 2654208
  111.5 44.4 %copy-start.2 = (f32[768]{0:T(1024)S(1)}, f32[768]{0:T(1024)}, u32[]{:S(2)}) copy-start(f32[768]{0:T(1024)} %param.8) | copy-start | bytes 9220
  111.5 44.4 %copy-start.3 = (f32[192]{0:T(256)S(1)}, f32[192]{0:T(256)}, u32[]{:S(2)}) copy-start(f32[192]{0:T(256)} %param.9) | copy-start | bytes 2308
  111.5 59.9 %copy-start.4 = (bf16[1536,768]{1,0:T(8,128)(2,1)S(1)}, bf16[1536,768]{1,0:T(8,128)(2,1)}, u32[]{:S(2)}) copy-start(bf16[1536,768]{1,0:T(8,128)(2,1)} %all-gather.4.cloned.1.call-done) | copy-start | bytes 7077892
  181.9 20.5 %all-to-all-start.6 = ((bf16[4,192,768]{2,1,0:T(8,128)(2,1)}), bf16[4,192,768]{2,1,0:T(8,128)(2,1)S(1)}, u32[]{:S(2)}, u32[]{:S(2)}) async-start(bf16[4,192,768]{2,1,0:T(8,128)(2,1)} %bitcast.13), calls=%async_computation.6 | async-start | bytes 2359296 | tf_op jit(solution)/shard_map/all_to_all | solution.py:25
  187.0 39.5 %all-gather.8.cloned.1.call-start = ((), (), s32[]{:S(2)}) async-start(), calls=%async_computation.13 | async-start | bytes 1474560 | tf_op jit(solution)/shard_map/all_gather | solution.py:44
  222.7 6.9 %all-to-all-start.8 = ((bf16[2,768,768]{2,1,0:T(8,128)(2,1)}), bf16[2,768,768]{2,1,0:T(8,128)(2,1)S(1)}, u32[]{:S(2)}, u32[]{:S(2)}) async-start(bf16[2,768,768]{2,1,0:T(8,128)(2,1)} %broadcast_in_dim.21), calls=%async_computation.8 | async-start | bytes 4718592 | tf_op jit(solution)/shard_map/all_to_all | solution.py:16
  226.5 48.9 %reduce-scatter.5.cloned.1.call-start = ((), (), s32[]{:S(2)}) async-start(), calls=%async_computation.14 | async-start | bytes 2654208 | tf_op jit(solution)/shard_map/reduce_scatter | solution.py:51
Sparse Core Ops, SparseCore 0:
  9.1 57.5 all-gather.3
  68.5 26.5 all-gather.5
  111.6 44.2 reduce-scatter.6
  189.3 24.6 all-gather.7
  234.4 40.9 reduce-scatter.4
